TPU v7x, 32 devices: a whole 2x2x4 slice. The times are simulated.
32 devices in a mesh: outer: 4 (over z), mid: 2 (over y), inner: 4 (over x, core).
Axes of the slice: x: 2, y: 2, z: 4, core: 2. Of those that a mesh axis runs over, the one named last changes fastest.
Arguments:
- x: bfloat16 [4096, 2048], P(('outer', 'mid', 'inner'))
- ids: int32 [4096, 6], P(('outer', 'mid', 'inner'))
- gates: float32 [4096, 6], P(('outer', 'mid', 'inner'))
- w1: bfloat16 [64, 2048, 1408], P(('outer', 'mid', 'inner'))
- w3: bfloat16 [64, 2048, 1408], P(('outer', 'mid', 'inner'))
- w2: bfloat16 [64, 1408, 2048], P(('outer', 'mid', 'inner'))
- ws1: bfloat16 [2048, 2816], replicated
- ws3: bfloat16 [2048, 2816], replicated
- ws2: bfloat16 [2816, 2048], replicated
Outputs:
- output: bfloat16 [4096, 2048], P(('outer', 'mid', 'inner'))
All inputs are finite; a program needn't handle non-finite values.
Results may differ from a plain program's by a relative error of at most 0.00633531.
Values are sent between devices in bfloat16 or wider.
A program may use at most 1 GiB of HBM per device.

v0:
```python
import jax
import jax.numpy as jnp
from jax import lax
from jax.sharding import PartitionSpec as P


def expert_rows(rows, lids, lg, w1, w3, w2, blk):
    nrow, top = lids.shape
    ne = w1.shape[0]
    key = jnp.where(lids >= 0, lids, ne).reshape(-1)
    order = jnp.argsort(key)
    counts = jnp.zeros((ne + 1,), jnp.int32).at[key].add(1)[:ne]
    starts = jnp.cumsum(counts) - counts
    ntile = (counts + blk - 1) // blk
    tend = jnp.cumsum(ntile)
    tstart = tend - ntile
    gflat = lg.reshape(-1)
    lanes = jnp.arange(blk)

    def body(i, acc):
        e = jnp.sum((tend <= i).astype(jnp.int32))
        r = (i - tstart[e]) * blk + lanes
        ok = r < counts[e]
        a = order[jnp.minimum(starts[e] + r, nrow * top - 1)]
        src = a // top
        g = jnp.where(ok, gflat[a], 0.0)
        xa = jnp.take(rows, src, axis=0)
        a1 = jnp.dot(xa, w1[e], preferred_element_type=jnp.float32)
        a3 = jnp.dot(xa, w3[e], preferred_element_type=jnp.float32)
        h = (jax.nn.silu(a1) * a3).astype(jnp.bfloat16)
        o = jnp.dot(h, w2[e], preferred_element_type=jnp.float32)
        return acc.at[src].add(g[:, None] * o)

    return lax.fori_loop(0, tend[-1], body, jnp.zeros((nrow, rows.shape[1]), jnp.float32))


def shared_ffn(x, ws1, ws3, ws2):
    s1 = jnp.dot(x, ws1, preferred_element_type=jnp.float32)
    s3 = jnp.dot(x, ws3, preferred_element_type=jnp.float32)
    hs = (jax.nn.silu(s1) * s3).astype(jnp.bfloat16)
    return jnp.dot(hs, ws2, preferred_element_type=jnp.float32)


def solution(mesh):
    axes = tuple(mesh.axis_names)
    nd = 1
    for a in axes:
        nd = nd * mesh.shape[a]
    tok = P(axes, None)
    wsp = P(axes, None, None)
    rep = P(None, None)

    def local(x, ids, gates, w1, w3, w2, ws1, ws3, ws2):
        t, hdim = x.shape
        top = ids.shape[1]
        epd = w1.shape[0]
        cap = min(t, 8 * ((2 * t * top + 8 * nd - 1) // (8 * nd)))
        blk = min(128, max(8, 8 * ((t * top // epd + 7) // 8)))
        devs = jnp.arange(nd)
        hit = jnp.any((ids // epd)[:, :, None] == devs[None, None, :], axis=1)
        pos = jnp.cumsum(hit.astype(jnp.int32), axis=0) - 1
        slot = jnp.where(hit, pos, cap)
        dst = jnp.broadcast_to(devs[None, :], (t, nd))
        tokid = jnp.broadcast_to(jnp.arange(t)[:, None], (t, nd))
        tok_of = jnp.full((nd, cap), t, jnp.int32).at[dst, slot].set(tokid, mode="drop")
        tc = jnp.minimum(tok_of, t - 1)
        sid = jnp.take(ids, tc, axis=0)
        mine = ((sid // epd) == devs[:, None, None]) & (tok_of < t)[:, :, None]
        send_x = jnp.take(x, tc, axis=0)
        send_id = jnp.where(mine, sid % epd, -1)
        send_g = jnp.where(mine, jnp.take(gates, tc, axis=0), 0.0)
        rx = lax.all_to_all(send_x, axes, 0, 0)
        rid = lax.all_to_all(send_id, axes, 0, 0)
        rg = lax.all_to_all(send_g, axes, 0, 0)
        out = expert_rows(rx.reshape(nd * cap, hdim), rid.reshape(nd * cap, top), rg.reshape(nd * cap, top), w1, w3, w2, blk)
        back = lax.all_to_all(out.astype(jnp.bfloat16).reshape(nd, cap, hdim), axes, 0, 0)
        moe = jnp.zeros((t, hdim), jnp.float32).at[tok_of.reshape(-1)].add(back.reshape(nd * cap, hdim).astype(jnp.float32), mode="drop")
        y = x.astype(jnp.float32) + shared_ffn(x, ws1, ws3, ws2) + moe
        return y.astype(jnp.bfloat16)

    return jax.shard_map(local, mesh=mesh, in_specs=(tok, tok, tok, wsp, wsp, wsp, rep, rep, rep), out_specs=tok, check_vma=False)
```

profile of v0, /device:TPU:0, one launch (start us, length us, event | category | flops | bytes accessed | tf_op | source)
XLA Modules:
  0.0 984.2 jit_solution(7585200132298970927)
XLA Ops:
  0.0 0.0 copy-start.2
  0.0 0.7 add_select_fusion.2
  0.7 0.8 copy.45
  1.6 1.9 copy.41
  3.4 1.8 copy.42
  5.2 1.9 compare_select_fusion.5
  7.1 2.7 copy.43
  9.8 0.0 copy-done.2
  9.8 0.1 multiply_reduce_fusion
  9.8 0.0 copy-done.3
  9.9 0.1 and_reduce_fusion
  9.9 0.1 copy.44
  10.0 0.1 reshape.346
  10.1 0.1 reshape.348
  10.2 15.5 %scatter_custom_fusion.3 = s32[1536]{0:T(1024)S(1)} fusion(s32[4096]{0:T(1024)S(1)} %reshape.346, s32[4096]{0:T(1024)S(1)} %reshape.348, s32[]{:T(128)} %constant.196.clone.1), kind=kCustom, calls=%fused_computation.92 | custom fusion | bytes 6148
  25.7 0.1 reshape.270
  25.9 0.1 reshape.300
  25.9 2.6 gather_fusion.3
  28.6 0.0 copy-start
  28.6 0.3 copy.46
  28.9 0.1 reshape.272
  29.0 0.2 fusion.54
  29.2 0.8 reshape.377
  29.9 7.4 all-to-all-start
  37.3 0.0 copy-done.1
  37.3 0.1 copy.49
  37.4 2.6 gather_fusion.4
  40.0 0.3 copy.50
  40.3 0.1 fusion.55
  40.5 0.8 reshape.379
  41.2 0.0 copy-done
  41.3 7.1 gather_fusion.5
  48.3 0.0 all-to-all-done
  48.3 5.8 all-to-all-start.1
  54.2 6.1 broadcast_select_fusion.4
  60.3 1.0 all-to-all-done.1
  61.3 5.1 all-to-all-start.2
  66.4 0.5 broadcast.480
  66.9 0.8 reduce.6
  67.7 0.1 reshape.378
  67.8 0.3 copy.47
  68.1 0.6 reshape.256
  68.7 0.5 reshape.261
  69.2 0.1 compare_select_fusion.6
  69.3 64.1 %scatter_custom_fusion.1 = s32[3]{0:T(128)S(1)} fusion(s32[9216]{0:T(1024)S(1)} %bitcast.96, s32[9216]{0:T(1024)S(1)} %broadcast.400, s32[]{:T(128)} %constant.198.clone.1), kind=kCustom, calls=%fused_computation.101 | custom fusion | flops 9216 | bytes 16 | tf_op jit(solution)/shard_map/scatter-add | solution.py:12
  133.4 0.2 reduce-window.14
  133.5 0.2 reduce-window.15
  133.7 0.5 broadcast.481
  134.2 0.8 reduce.7
  135.0 0.1 reshape.380
  135.1 0.3 copy.51
  135.4 0.5 reshape_reshape.3
  136.0 0.6 slice.8
  136.6 8.8 sort.17
  145.4 53.2 %all-to-all-done.2 = bf16[32,48,2048]{2,1,0:T(8,128)(2,1)} async-done(((bf16[32,48,2048]{2,1,0:T(8,128)(2,1)}), bf16[32,48,2048]{2,1,0:T(8,128)(2,1)}, u32[]{:S(2)}, u32[]{:S(2)}) %all-to-all-start.2) | async-done | bytes 6291488 | tf_op jit(solution)/shard_map/all_to_all | solution.py:72
  198.7 6.2 broadcast_in_dim.100
  204.8 0.8 while.13
  205.7 8.2 convert_element_type.41
  213.8 615.3 %all-to-all-start.3 = ((bf16[32,48,2048]{2,1,0:T(8,128)(2,1)}), bf16[32,48,2048]{2,1,0:T(8,128)(2,1)}, u32[]{:S(2)}, u32[]{:S(2)}) async-start(bf16[32,48,2048]{2,1,0:T(8,128)(2,1)} %bitcast.89), calls=%async_computation.3 | async-start | bytes 12582912 | tf_op jit(solution)/shard_map/all_to_all | solution.py:76
  829.2 5.9 fusion.56
  835.1 11.1 %convolution_add_fusion = f32[128,2048]{1,0:T(8,128)S(1)} fusion(bf16[2816,2048]{1,0:T(8,128)(2,1)} %param.19, bf16[128,2048]{1,0:T(8,128)(2,1)S(1)} %copy-done, bf16[2048,2816]{1,0:T(8,128)(2,1)} %param.18, f32[128,2816]{1,0:T(8,128)S(1)} %fusion.56), kind=kOutput, calls=%fused_computation.57 | convolution fusion | flops 2955476992 | bytes 26083328 | tf_op jit(solution)/shard_map/dot_general | solution.py:41
  846.2 115.2 %all-to-all-done.3 = bf16[32,48,2048]{2,1,0:T(8,128)(2,1)} async-done(((bf16[32,48,2048]{2,1,0:T(8,128)(2,1)}), bf16[32,48,2048]{2,1,0:T(8,128)(2,1)}, u32[]{:S(2)}, u32[]{:S(2)}) %all-to-all-start.3) | async-done | bytes 6291488 | tf_op jit(solution)/shard_map/all_to_all | solution.py:76
  961.4 21.5 %scatter_custom_fusion.2 = f32[128,2048]{1,0:T(8,128)S(1)} fusion(f32[128,2048]{1,0:T(8,128)S(1)} %convolution_add_fusion, s32[1536]{0:T(1024)S(1)} %fusion.45, bf16[1536,2048]{1,0:T(8,128)(2,1)} %bitcast.24), kind=kCustom, calls=%fused_computation.51 | custom fusion | flops 6291456 | bytes 7340032 | tf_op jit(solution)/shard_map/scatter-add | solution.py:77
  982.9 0.9 convert_element_type.44
  (18 shorter events, 0.1 us)
Async XLA Ops:
  0.0 9.8 copy-start.2
  0.0 9.8 %copy-start.3 = (s32[2]{0:T(128)S(1)}, s32[2]{0:T(128)}, u32[]{:S(2)}) copy-start(s32[2]{0:T(128)} %constant.216) | copy-start | bytes 28
  7.1 30.2 %copy-start.1 = (f32[128,6]{0,1:T(8,128)S(1)}, f32[128,6]{0,1:T(8,128)}, u32[]{:S(2)}) copy-start(f32[128,6]{0,1:T(8,128)} %param.13) | copy-start | bytes 9220
  28.6 12.7 %copy-start = (bf16[128,2048]{1,0:T(8,128)(2,1)S(1)}, bf16[128,2048]{1,0:T(8,128)(2,1)}, u32[]{:S(2)}) copy-start(bf16[128,2048]{1,0:T(8,128)(2,1)} %param.11) | copy-start | bytes 1572868
  29.9 18.4 %all-to-all-start = ((s32[32,1,288]{2,1,0:T(1,128)}), s32[32,1,288]{2,1,0:T(1,128)S(1)}, u32[]{:S(2)}, u32[]{:S(2)}) async-start(s32[32,1,288]{2,1,0:T(1,128)} %reshape.377), calls=%async_computation | async-start | bytes 98304 | tf_op jit(solution)/shard_map/all_to_all | solution.py:73
  48.3 13.0 %all-to-all-start.1 = ((f32[32,1,288]{2,1,0:T(1,128)}), f32[32,1,288]{2,1,0:T(1,128)S(1)}, u32[]{:S(2)}, u32[]{:S(2)}) async-start(f32[32,1,288]{2,1,0:T(1,128)} %reshape.379), calls=%async_computation.1 | async-start | bytes 98304 | tf_op jit(solution)/shard_map/all_to_all | solution.py:74
  61.3 137.3 %all-to-all-start.2 = ((bf16[32,48,2048]{2,1,0:T(8,128)(2,1)}), bf16[32,48,2048]{2,1,0:T(8,128)(2,1)}, u32[]{:S(2)}, u32[]{:S(2)}) async-start(bf16[32,48,2048]{2,1,0:T(8,128)(2,1)} %broadcast_select_fusion.4), calls=%async_computation.2 | async-start | bytes 12582912 | tf_op jit(solution)/shard_map/all_to_all | solution.py:72
  213.8 747.6 %all-to-all-start.3 = ((bf16[32,48,2048]{2,1,0:T(8,128)(2,1)}), bf16[32,48,2048]{2,1,0:T(8,128)(2,1)}, u32[]{:S(2)}, u32[]{:S(2)}) async-start(bf16[32,48,2048]{2,1,0:T(8,128)(2,1)} %bitcast.89), calls=%async_computation.3 | async-start | bytes 12582912 | tf_op jit(solution)/shard_map/all_to_all | solution.py:76
where the time goes:
time: 983 us; the launch traced here: 984 us
  starting transfers between devices  634 us (64%)
  waiting for transfers between devices  169 us (17%)
  other arithmetic  115 us (12%)
  local copies, waits for them, and re-layouts  48 us (5%)
  matrix products  17 us (2%)
    all_to_all x1, starting transfers between devices, local(): lax.all_to_all(out.astype(jnp.bfloat16).reshape(nd, cap, hdim), axes, 0, 0)  615 us
    all_to_all x1, waiting for transfers between devices, local(): lax.all_to_all(out.astype(jnp.bfloat16).reshape(nd, cap, hdim), axes, 0, 0)  115 us
    scatter-add x1, other arithmetic, expert_rows(): counts = jnp.zeros((ne + 1,), jnp.int32).at[key].add(1)[:ne]  64.1 us
    all_to_all x1, waiting for transfers between devices, local(): rx = lax.all_to_all(send_x, axes, 0, 0)  53.2 us
    scatter-add x1, other arithmetic, local(): jnp.zeros((t, hdim), jnp.float32).at[tok_of.reshape(-1)]  21.5 us
  transfers between devices with their start and end apart: 4, of which 3 were waited for; matrix products, arithmetic and copies ran while one was open for 11% of the time, Pallas kernels for 0%

commit v1 on v0

v1 whole, which is shorter than its diff:
```python
import functools

import jax
import jax.numpy as jnp
from jax import lax
from jax.experimental import pallas as pl
from jax.experimental.pallas import tpu as pltpu
from jax.sharding import PartitionSpec as P

CAP = 48
TN = 256
MESH = pl.DeviceIdType.MESH
F32 = jnp.float32
BF16 = jnp.bfloat16


def cut(text, n):
    return [text[i:i + n] for i in range(0, len(text), n)]


def rel(name):
    return int(name[1]) * 4 + "CXYD".index(name[0])


class Place:
    def __init__(self, axes):
        o, m, i = axes
        self.axes = axes
        self.z = lax.axis_index(o)
        self.y = lax.axis_index(m)
        inner = lax.axis_index(i)
        self.x = inner // 2
        self.c = inner % 2
        self.me = self.z * 8 + self.y * 4 + inner
        self.mate = self.me + 1 - 2 * self.c
        self.mid = jnp.logical_and(self.z >= 1, self.z <= 2)
        self.z1 = self.z + 1 - 2 * (self.z % 2)
        self.z3 = 3 - self.z

    def dev(self, z, y, x, c):
        o, m, i = self.axes
        return {o: z, m: y, i: x * 2 + c}

    def target(self, name):
        z, y, x, c = self.z, self.y, self.x, self.c
        return {
            "X": self.dev(z, y, 1 - x, c),
            "Y": self.dev(z, 1 - y, x, c),
            "P": self.dev(z, y, x, 1 - c),
            "Z1": self.dev(self.z1, y, x, c),
            "Z3": self.dev(self.z3, y, x, c),
        }[name]


FLIP = {"X": 1, "Y": 2, "Z1": 4, "Z3": 12, "P": 0}


def barrier(pos):
    sem = pltpu.get_barrier_semaphore()
    for t in ("X", "Y", "P", "Z1"):
        pl.semaphore_signal(sem, inc=1, device_id=pos.target(t), device_id_type=MESH)

    @pl.when(pos.mid)
    def _():
        pl.semaphore_signal(sem, inc=1, device_id=pos.target("Z3"), device_id_type=MESH)
        pl.semaphore_wait(sem, 5)

    @pl.when(jnp.logical_not(pos.mid))
    def _():
        pl.semaphore_wait(sem, 4)


def slots(meta, dev, tri):
    ids = meta[0:8, :]
    gat = meta[8:16, :]
    e0 = (2 * dev).astype(F32)
    m0 = ids == e0
    m1 = ids == e0 + 1.0
    g0 = jnp.sum(jnp.where(m0, gat, 0.0), axis=0, keepdims=True)
    g1 = jnp.sum(jnp.where(m1, gat, 0.0), axis=0, keepdims=True)
    hit = jnp.sum(jnp.where(m0, 1.0, 0.0) + jnp.where(m1, 1.0, 0.0), axis=0, keepdims=True) > 0.5
    hitf = jnp.broadcast_to(jnp.where(hit, 1.0, 0.0), (8, ids.shape[1])).astype(BF16)
    pos = jnp.dot(hitf, tri, preferred_element_type=F32)[0:1, :]
    row = lax.broadcasted_iota(jnp.int32, (CAP, ids.shape[1]), 0).astype(F32)
    oh = jnp.where(jnp.logical_and(row == pos, jnp.where(hit, 1.0, 0.0) > 0.5), 1.0, 0.0)
    return oh, g0, g1


def strict_upper(t):
    a = lax.broadcasted_iota(jnp.int32, (t, t), 0)
    b = lax.broadcasted_iota(jnp.int32, (t, t), 1)
    return jnp.where(a < b, 1.0, 0.0).astype(BF16)


GROUPS = [cut(g, 2) for g in ("C0X0Y0C1", "X1Y1C2C3", "X2Y2D0D1", "X3Y3D2D3")]
EVENTS = {
    1: "C1XC1YC13C31Y0XY0PX0PC1P",
    2: "C2XC2YC21X1YX1PY1PC2P",
    3: "C3XC3YY2XY2PD0PC3P",
    4: "X2PD1P",
    5: "X3YX3PY3P",
    6: "D2PD3P",
}


def expert_kernel(axes, x_ref, m_ref, w1_ref, w3_ref, w2_ref, os_ref, op_ref, mo_ref,
                  xall, mall, w13, w2v, xg, hbuf, gbuf, obuf,
                  xs, xr, ms, mr, ls, ws, w2s, osem, pss, prs):
    pos = Place(axes)
    t, hdim = x_ref.shape
    nf = w1_ref.shape[2] // 128
    nn = hdim // TN
    barrier(pos)
    sends = []

    def send(b, name, own=False):
        dst = rel(b) ^ FLIP[name]
        dc = int(name == "P")
        n = len(sends)

        def make():
            out = []
            for ref, full, ss, rs in ((m_ref, mall, ms, mr), (x_ref, xall, xs, xr)):
                src = ref if own else full.at[0, rel(b)]
                out.append(pltpu.make_async_remote_copy(src, full.at[dc, dst], ss.at[n], rs.at[dc, dst],
                                                        device_id=pos.target(name), device_id_type=MESH))
            return out
        for c in make():
            c.start()
        sends.append(make)

    def arrived(b, dc):
        for ref, full, ss, rs in ((m_ref, mall, ms, mr), (x_ref, xall, xs, xr)):
            pltpu.make_async_remote_copy(ref, full.at[dc, rel(b)], ss.at[0], rs.at[dc, rel(b)],
                                         device_id=pos.target("X"), device_id_type=MESH).wait_recv()

    mid_sends = []

    def mid_send(b, name, own=False):
        pl.when(pos.mid)(lambda: send(b, name, own))
        mid_sends.append(len(sends) - 1)

    for name in ("X", "Y", "Z1"):
        send("C0", name, True)
    mid_send("C0", "Z3", True)
    send("C0", "P", True)
    lx = pltpu.make_async_copy(x_ref, xall.at[0, 0], ls.at[0])
    lm = pltpu.make_async_copy(m_ref, mall.at[0, 0], ls.at[1])
    lx.start()
    lm.start()

    def w13_copy(i, half):
        e, j = i // nf, i % nf
        src = w1_ref if half == 0 else w3_ref
        return pltpu.make_async_copy(src.at[e, :, pl.ds(pl.multiple_of(j * 128, 128), 128)],
                                     w13.at[i, :, pl.ds(half * 128, 128)], ws.at[half, i])

    def w2_copy(i):
        e, n = i // nn, i % nn
        return pltpu.make_async_copy(w2_ref.at[e, :, pl.ds(pl.multiple_of(n * TN, TN), TN)], w2v.at[i], w2s.at[i])

    def start_w13(i, _):
        w13_copy(i, 0).start()
        w13_copy(i, 1).start()
        return 0

    def start_w2(i, _):
        w2_copy(i).start()
        return 0

    lax.fori_loop(0, 2 * nf, start_w13, 0)
    lax.fori_loop(0, 2 * nn, start_w2, 0)

    seen = set()

    def event(n):
        for step in cut(EVENTS[n], 3):
            b, to = step[:2], step[2]
            if b == "C3" and n == 1:
                pl.when(pos.mid)(lambda: arrived(b, 0))
            elif b == "C3" and b not in seen:
                pl.when(jnp.logical_not(pos.mid))(lambda: arrived(b, 0))
                seen.add(b)
            elif b not in seen:
                arrived(b, 0)
                seen.add(b)
            if to in "13":
                mid_send(b, "Z" + to)
            else:
                send(b, to)

    tri = strict_upper(t)
    outs = {}

    def gather_rows(group):
        for i, b in enumerate(group):
            for dc in range(2):
                if dc == 1:
                    arrived(b, 1)
                s = rel(b)
                oh, g0, g1 = slots(mall[dc, s], pos.me, tri)
                r0 = (dc * 4 + i) * CAP
                xg[r0:r0 + CAP, :] = jnp.dot(oh.astype(BF16), xall[dc, s], preferred_element_type=F32).astype(BF16)
                gbuf[0, r0:r0 + CAP, :] = jnp.broadcast_to(jnp.sum(oh * g0, axis=1, keepdims=True), (CAP, 128))
                gbuf[1, r0:r0 + CAP, :] = jnp.broadcast_to(jnp.sum(oh * g1, axis=1, keepdims=True), (CAP, 128))

    def up(e, first):
        def body(j, _):
            i = e * nf + j
            if first:
                w13_copy(i, 0).wait()
                w13_copy(i, 1).wait()
            a = jnp.dot(xg[...], w13[i], preferred_element_type=F32)
            h = (jax.nn.silu(a[:, :128]) * a[:, 128:]).astype(BF16)
            hbuf[e, :, pl.ds(pl.multiple_of(j * 128, 128), 128)] = h
            return 0
        lax.fori_loop(0, nf, body, 0)

    def down(g, first):
        def body(n, _):
            if first:
                w2_copy(n).wait()
                w2_copy(nn + n).wait()
            o0 = jnp.dot(hbuf[0], w2v[n], preferred_element_type=F32)
            o1 = jnp.dot(hbuf[1], w2v[nn + n], preferred_element_type=F32)
            o = gbuf[0, :, 0:1] * o0 + gbuf[1, :, 0:1] * o1
            obuf[g % 2, :, pl.ds(pl.multiple_of(n * TN, TN), TN)] = o.astype(BF16)
            return 0
        lax.fori_loop(0, nn, body, 0)

    def put(g):
        outs[g] = []
        for i, b in enumerate(GROUPS[g]):
            s = rel(b)
            q = 4 * g + i
            a = pltpu.make_async_copy(obuf.at[g % 2, pl.ds(i * CAP, CAP), :], os_ref.at[s], osem.at[q])
            r = pltpu.make_async_remote_copy(obuf.at[g % 2, pl.ds((4 + i) * CAP, CAP), :], op_ref.at[s], pss.at[q],
                                             prs.at[q], device_id=pos.target("P"), device_id_type=MESH)
            r.start()
            a.start()
            outs[g].append((a, r))

    def put_done(g):
        for a, r in outs[g]:
            a.wait()
            r.wait_send()

    event(1)
    lx.wait()
    lm.wait()
    gather_rows(GROUPS[0])
    up(0, True)
    up(1, True)
    event(2)
    down(0, True)
    put(0)
    event(3)
    gather_rows(GROUPS[1])
    up(0, False)
    up(1, False)
    event(4)
    down(1, False)
    put(1)
    gather_rows(GROUPS[2])
    up(0, False)
    event(5)
    up(1, False)
    put_done(0)
    down(2, False)
    put(2)
    event(6)
    gather_rows(GROUPS[3])
    up(0, False)
    up(1, False)
    put_done(1)
    down(3, False)
    put(3)
    mo_ref[...] = mall[0]
    for n, make in enumerate(sends):
        def done(make=make):
            for c in make():
                c.wait_send()
        if n in mid_sends:
            pl.when(pos.mid)(done)
        else:
            done()
    put_done(2)
    put_done(3)
    for g in range(4):
        for a, r in outs[g]:
            r.wait_recv()


SLOTS = cut("dX3dX1dY2dY0cX0cX1cX2cX3cY0cY1cY2cY3az0az2az3bz0bz1", 3)
HOPS = {"1": "bz1az0az0", "2": "az2bz1az3", "3": "az3bz0az2"}


def combine_kernel(axes, os_ref, op_ref, m_ref, x_ref, v1_ref, v3_ref, v2_ref, y_ref,
                   ov, sbuf, rbuf, w13, w2v, hs, sh, xv,
                   osem, ssem, rsem, ws, w2s, ls):
    pos = Place(axes)
    t, hdim = x_ref.shape
    nf = v1_ref.shape[1] // 128
    nn = hdim // TN
    order = [rel(b) for b in cut("D3D2D1D0X3Y3X2Y2X1Y1X0Y0C3C2C1C0", 2)]

    def o_copy(s, h):
        src = os_ref if h == 0 else op_ref
        return pltpu.make_async_copy(src.at[s], ov.at[s, pl.ds(h * CAP, CAP), :], osem.at[h, s])

    for s in order:
        o_copy(s, 0).start()
        o_copy(s, 1).start()
    lx = pltpu.make_async_copy(x_ref, xv, ls.at[0])
    lx.start()

    def w13_copy(i, half):
        src = v1_ref if half == 0 else v3_ref
        return pltpu.make_async_copy(src.at[:, pl.ds(pl.multiple_of(i * 128, 128), 128)],
                                     w13.at[i, :, pl.ds(half * 128, 128)], ws.at[half, i])

    def w2_copy(n):
        return pltpu.make_async_copy(v2_ref.at[:, pl.ds(pl.multiple_of(n * TN, TN), TN)], w2v.at[n], w2s.at[n])

    def start_w13(i, _):
        w13_copy(i, 0).start()
        w13_copy(i, 1).start()
        return 0

    def start_w2(i, _):
        w2_copy(i).start()
        return 0

    lax.fori_loop(0, nf, start_w13, 0)
    lax.fori_loop(0, nn, start_w2, 0)
    barrier(pos)
    tri = strict_upper(t)

    def contrib(s):
        o_copy(s, 0).wait()
        o_copy(s, 1).wait()
        a, _, _ = slots(m_ref[s], pos.me, tri)
        b, _, _ = slots(m_ref[s], pos.mate, tri)
        ab = jnp.concatenate([a, b], axis=0).T.astype(BF16)
        return jnp.dot(ab, ov[s], preferred_element_type=F32)

    def copy(i, n, name):
        return pltpu.make_async_remote_copy(sbuf.at[i], rbuf.at[n], ssem.at[i], rsem.at[n],
                                            device_id=pos.target(name), device_id_type=MESH)

    def got(name):
        copy(0, slot[name], "X").wait_recv()
        return rbuf[slot[name]].astype(F32)

    slot = {name: n for n, name in enumerate(SLOTS)}
    used = []

    def emit(val, name, to):
        i = len(used)
        sbuf[i] = val.astype(BF16)
        c = copy(i, slot[name], to)
        c.start()
        used.append(c)

    for b, to in zip(cut("D3D2D1D0", 2), "XYXY"):
        emit(contrib(rel(b)), "d" + to + b[1], to)

    def column(k):
        for to, other in (("X", "Y"), ("Y", "X")):
            v = contrib(rel(to + k))
            if "d" + other + k in slot:
                v = v + got("d" + other + k)
            emit(v, "c" + to + k, to)

    def share_up(lo, hi):
        def body(i, _):
            w13_copy(i, 0).wait()
            w13_copy(i, 1).wait()
            a = jnp.dot(xv[...], w13[i], preferred_element_type=F32)
            hs[:, pl.ds(pl.multiple_of(i * 128, 128), 128)] = (jax.nn.silu(a[:, :128]) * a[:, 128:]).astype(BF16)
            return 0
        lax.fori_loop(lo, hi, body, 0)

    def share_down():
        def body(n, _):
            w2_copy(n).wait()
            cols = pl.ds(pl.multiple_of(n * TN, TN), TN)
            sh[:, cols] = xv[:, cols].astype(F32) + jnp.dot(hs[...], w2v[n], preferred_element_type=F32)
            return 0
        lax.fori_loop(0, nn, body, 0)

    zs = []

    def along(k):
        v = contrib(rel("C" + k)) + got("cX" + k) + got("cY" + k)
        i = len(used) + len(zs)
        mid_in, mid_to, end_to = cut(HOPS[k], 3)
        link = "Z1" if mid_to[0] == "a" else "Z3"

        @pl.when(pos.mid)
        def _():
            sbuf[i] = (v + got(mid_in)).astype(BF16)
            copy(i, slot[mid_to], link).start()

        @pl.when(jnp.logical_not(pos.mid))
        def _():
            sbuf[i] = v.astype(BF16)
            copy(i, slot[end_to], "Z1").start()
        zs.append(i)

    for k in "3210":
        column(k)
    lx.wait()
    share_up(0, nf)
    along("3")
    share_down()
    along("2")
    along("1")
    v = sh[...] + contrib(rel("C0")) + got("cX0") + got("cY0") + got("az0")
    sh[...] = v

    @pl.when(pos.mid)
    def _():
        y_ref[...] = (sh[...] + got("bz0")).astype(BF16)

    @pl.when(jnp.logical_not(pos.mid))
    def _():
        y_ref[...] = sh[...].astype(BF16)
    for c in used:
        c.wait_send()
    for i in zs:
        copy(i, 0, "X").wait_send()


VLIM = 67043328


def solution(mesh):
    axes = tuple(mesh.axis_names)
    tok = P(axes, None)
    wsp = P(axes, None, None)
    rep = P(None, None)
    ANY = pl.BlockSpec(memory_space=pl.ANY)
    VM = pl.BlockSpec(memory_space=pltpu.VMEM)

    def local(x, ids, gates, w1, w3, w2, ws1, ws3, ws2):
        t, hdim = x.shape
        top = ids.shape[1]
        f = w1.shape[2]
        fs = ws1.shape[1]
        nch = mesh.size // 2
        rows = 8 * CAP
        pad = ((0, 8 - top), (0, 0))
        meta = jnp.concatenate([jnp.pad(ids.T.astype(F32), pad, constant_values=-1.0), jnp.pad(gates.T, pad)], axis=0)
        dma = pltpu.SemaphoreType.DMA
        nsend = 40
        o_same, o_mate, m_same = pl.pallas_call(
            functools.partial(expert_kernel, axes),
            name="experts",
            out_shape=(
                jax.ShapeDtypeStruct((nch, CAP, hdim), BF16),
                jax.ShapeDtypeStruct((nch, CAP, hdim), BF16),
                jax.ShapeDtypeStruct((nch, 16, t), F32),
            ),
            in_specs=[ANY] * 5,
            out_specs=(ANY, ANY, VM),
            scratch_shapes=[
                pltpu.VMEM((2, nch, t, hdim), BF16),
                pltpu.VMEM((2, nch, 16, t), F32),
                pltpu.VMEM((2 * f // 128, hdim, 256), BF16),
                pltpu.VMEM((2 * hdim // TN, f, TN), BF16),
                pltpu.VMEM((rows, hdim), BF16),
                pltpu.VMEM((2, rows, f), BF16),
                pltpu.VMEM((2, rows, 128), F32),
                pltpu.VMEM((2, rows, hdim), BF16),
                dma((nsend,)), dma((2, nch)), dma((nsend,)), dma((2, nch)),
                dma((2,)), dma((2, 2 * f // 128)), dma((2 * hdim // TN,)),
                dma((nch,)), dma((nch,)), dma((nch,)),
            ],
            compiler_params=pltpu.CompilerParams(collective_id=0, has_side_effects=True, vmem_limit_bytes=VLIM),
        )(x, meta, w1, w3, w2)
        y = pl.pallas_call(
            functools.partial(combine_kernel, axes),
            name="combine",
            out_shape=jax.ShapeDtypeStruct((t, hdim), BF16),
            in_specs=[ANY, ANY, VM, ANY, ANY, ANY, ANY],
            out_specs=VM,
            scratch_shapes=[
                pltpu.VMEM((nch, 2 * CAP, hdim), BF16),
                pltpu.VMEM((15, t, hdim), BF16),
                pltpu.VMEM((17, t, hdim), BF16),
                pltpu.VMEM((fs // 128, hdim, 256), BF16),
                pltpu.VMEM((hdim // TN, fs, TN), BF16),
                pltpu.VMEM((t, fs), BF16),
                pltpu.VMEM((t, hdim), F32),
                pltpu.VMEM((t, hdim), BF16),
                dma((2, nch)), dma((15,)), dma((17,)),
                dma((2, fs // 128)), dma((hdim // TN,)), dma((1,)),
            ],
            compiler_params=pltpu.CompilerParams(collective_id=1, has_side_effects=True, vmem_limit_bytes=VLIM),
        )(o_same, o_mate, m_same, x, ws1, ws3, ws2)
        return y

    return jax.shard_map(local, mesh=mesh, in_specs=(tok, tok, tok, wsp, wsp, wsp, rep, rep, rep), out_specs=tok, check_vma=False)
```

time: 983 us -> 222 us (0.23)
  starting transfers between devices: 634 us -> 0 us
  Pallas kernels: 0 us -> 218 us
  waiting for transfers between devices: 169 us -> 0 us
  other arithmetic: 115 us -> 1.98 us
  local copies, waits for them, and re-layouts: 48 us -> 1.88 us
  matrix products: 17 us -> 0 us
    all_to_all x4 -> x0, starting transfers between devices: 634 us -> none  [the longest x1 615 us: local(): lax.all_to_all(out.astype(jnp.bfloat16).reshape(nd, cap, hdim), axes, 0, 0)]
    pallas_call x0 -> x2, Pallas kernels: none -> 218 us  [the longest x1 119 us: local(): pl.pallas_call(functools.partial(expert_kernel, axes), name='experts', ou...]
    all_to_all x4 -> x0, waiting for transfers between devices: 169 us -> none  [the longest x1 115 us: local(): lax.all_to_all(out.astype(jnp.bfloat16).reshape(nd, cap, hdim), axes, 0, 0)]
    scatter-add x2 -> x0, other arithmetic: 85.6 us -> none  [the longest x1 64.1 us: expert_rows(): counts = jnp.zeros((ne + 1,), jnp.int32).at[key].add(1)[:ne]]
    dot_general x2 -> x0, matrix products: 17 us -> none  [the longest x1 11.1 us: shared_ffn(): return jnp.dot(hs, ws2, preferred_element_type=jnp.float32)]
    unnamed x17 -> x1, local copies, waits for them, and re-layouts: 18.3 us -> 1.88 us
    gather x5 -> x0, local copies, waits for them, and re-layouts: 12.9 us -> none  [the longest x1 7.09 us: local(): send_x = jnp.take(x, tc, axis=0)]
  transfers between devices with their start and end apart: 4 -> 0, of which waited for: 3 -> 0; matrix products, arithmetic and copies ran while one was open for 11% -> 0% of each run, Pallas kernels for 0% -> 0%
where the time goes in v1:
time: 222 us
  Pallas kernels  218 us (98%)
    pallas_call x1, Pallas kernels, local(): pl.pallas_call(functools.partial(expert_kernel, axes), name='experts', ou...  119 us
    pallas_call x1, Pallas kernels, local(): pl.pallas_call(functools.partial(combine_kernel, axes), name='combine', o...  98.7 us

profile of v1, /device:TPU:0, one launch (start us, length us, event | category | flops | bytes accessed | tf_op | source)
XLA Modules:
  0.0 221.7 jit_solution(15147771427628886600)
XLA Ops:
  0.0 0.7 convert_bitcast_fusion
  0.7 1.3 select_maximum_fusion.m_ref
  2.0 119.1 %experts.1 = (bf16[16,48,2048]{2,1,0:T(8,128)(2,1)}, bf16[16,48,2048]{2,1,0:T(8,128)(2,1)}, f32[16,16,128]{2,1,0:T(8,128)}) custom-call(bf16[128,2048]{1,0:T(8,128)(2,1)} %x_ref.3, f32[16,128]{1,0:T(8,128)} %select_maximum_fusion.m_ref, bf16[2,2048,1408]{2,1,0:T(8,128)(2,1)} %w1_ref.1, bf16[2,2048,1408]{2,1,0:T(8,128)(2,1)} %w3_ref.1, ...), custom_call_target="tpu_custom_call" | custom-call | tf_op jit(solution)/shard_map/experts/pallas_call | solution.py:457
  121.1 98.7 %combine.1 = bf16[128,2048]{1,0:T(8,128)(2,1)} custom-call(bf16[16,48,2048]{2,1,0:T(8,128)(2,1)} %get-tuple-element.8.os_ref, bf16[16,48,2048]{2,1,0:T(8,128)(2,1)} %get-tuple-element.9.op_ref, f32[16,16,128]{2,1,0:T(8,128)} %get-tuple-element.10.m_ref, bf16[128,2048]{1,0:T(8,128)(2,1)} %x_ref.3, bf16[2048,2816]{1,0:T(8,128)(2,1)} %v1_ref.1, ...), custom_call_target="tpu_custom_call" | custom-call | tf_op jit(solution)/shard_map/combine/pallas_call | solution.py:482
  219.8 1.9 copy.11

commit v2 on v1

--- a/solution.py
+++ b/solution.py
@@ -8,7 +8,8 @@
 from jax.sharding import PartitionSpec as P
 
 CAP = 48
-TN = 256
+TN = 512
+MOST = 4
 MESH = pl.DeviceIdType.MESH
 F32 = jnp.float32
 BF16 = jnp.bfloat16
@@ -33,6 +34,7 @@
         self.c = inner % 2
         self.me = self.z * 8 + self.y * 4 + inner
         self.mate = self.me + 1 - 2 * self.c
+        self.chip = {"X": self.me + 2 - 4 * self.x, "Y": self.me + 4 - 8 * self.y}
         self.mid = jnp.logical_and(self.z >= 1, self.z <= 2)
         self.z1 = self.z + 1 - 2 * (self.z % 2)
         self.z3 = 3 - self.z
@@ -92,7 +94,8 @@
     return jnp.where(a < b, 1.0, 0.0).astype(BF16)
 
 
-GROUPS = [cut(g, 2) for g in ("C0X0Y0C1", "X1Y1C2C3", "X2Y2D0D1", "X3Y3D2D3")]
+GROUPS = [cut(g, 2) for g in ("C0X0Y0C1", "X1Y1C2", "C3Y2D0", "X2D1X3Y3", "D2D3")]
+WHEN = ("1__2", "__3", "__4", "5__6", "__")
 EVENTS = {
     1: "C1XC1YC13C31Y0XY0PX0PC1P",
     2: "C2XC2YC21X1YX1PY1PC2P",
@@ -153,7 +156,7 @@
         e, j = i // nf, i % nf
         src = w1_ref if half == 0 else w3_ref
         return pltpu.make_async_copy(src.at[e, :, pl.ds(pl.multiple_of(j * 128, 128), 128)],
-                                     w13.at[i, :, pl.ds(half * 128, 128)], ws.at[half, i])
+                                     w13.at[j, :, pl.ds(pl.multiple_of(e * 256 + half * 128, 128), 128)], ws.at[half, i])
 
     def w2_copy(i):
         e, n = i // nn, i % nn
@@ -193,49 +196,51 @@
     outs = {}
 
     def gather_rows(group):
-        for i, b in enumerate(group):
-            for dc in range(2):
-                if dc == 1:
-                    arrived(b, 1)
-                s = rel(b)
-                oh, g0, g1 = slots(mall[dc, s], pos.me, tri)
-                r0 = (dc * 4 + i) * CAP
-                xg[r0:r0 + CAP, :] = jnp.dot(oh.astype(BF16), xall[dc, s], preferred_element_type=F32).astype(BF16)
-                gbuf[0, r0:r0 + CAP, :] = jnp.broadcast_to(jnp.sum(oh * g0, axis=1, keepdims=True), (CAP, 128))
-                gbuf[1, r0:r0 + CAP, :] = jnp.broadcast_to(jnp.sum(oh * g1, axis=1, keepdims=True), (CAP, 128))
-
-    def up(e, first):
+        for b in group:
+            arrived(b, 1)
+        for dc in range(2):
+            for i, b in enumerate(group):
+                oh, g0, g1 = slots(mall[dc, rel(b)], pos.me, tri)
+                r0 = (dc * len(group) + i) * CAP
+                rows = slice(r0, r0 + CAP)
+                xg[rows, :] = jnp.dot(oh.astype(BF16), xall[dc, rel(b)], preferred_element_type=F32).astype(BF16)
+                for e, g in enumerate((g0, g1)):
+                    gbuf[e, rows, :] = jnp.broadcast_to(jnp.sum(oh * g, axis=1, keepdims=True), (CAP, 128))
+
+    def up(m, lo, hi, first):
         def body(j, _):
-            i = e * nf + j
             if first:
-                w13_copy(i, 0).wait()
-                w13_copy(i, 1).wait()
-            a = jnp.dot(xg[...], w13[i], preferred_element_type=F32)
-            h = (jax.nn.silu(a[:, :128]) * a[:, 128:]).astype(BF16)
-            hbuf[e, :, pl.ds(pl.multiple_of(j * 128, 128), 128)] = h
+                for e in range(2):
+                    w13_copy(e * nf + j, 0).wait()
+                    w13_copy(e * nf + j, 1).wait()
+            aa = jnp.dot(xg[:m, :], w13[j], preferred_element_type=F32)
+            for e in range(2):
+                a1 = aa[:, e * 256:e * 256 + 128]
+                a3 = aa[:, e * 256 + 128:e * 256 + 256]
+                hbuf[e, :m, pl.ds(pl.multiple_of(j * 128, 128), 128)] = (jax.nn.silu(a1) * a3).astype(BF16)
             return 0
-        lax.fori_loop(0, nf, body, 0)
-
-    def down(g, first):
+        lax.fori_loop(lo, hi, body, 0)
+
+    def down(m, par, first):
         def body(n, _):
             if first:
                 w2_copy(n).wait()
                 w2_copy(nn + n).wait()
-            o0 = jnp.dot(hbuf[0], w2v[n], preferred_element_type=F32)
-            o1 = jnp.dot(hbuf[1], w2v[nn + n], preferred_element_type=F32)
-            o = gbuf[0, :, 0:1] * o0 + gbuf[1, :, 0:1] * o1
-            obuf[g % 2, :, pl.ds(pl.multiple_of(n * TN, TN), TN)] = o.astype(BF16)
+            o0 = jnp.dot(hbuf[0, :m, :], w2v[n], preferred_element_type=F32)
+            o1 = jnp.dot(hbuf[1, :m, :], w2v[nn + n], preferred_element_type=F32)
+            o = gbuf[0, :m, 0:1] * o0 + gbuf[1, :m, 0:1] * o1
+            obuf[par, :m, pl.ds(pl.multiple_of(n * TN, TN), TN)] = o.astype(BF16)
             return 0
         lax.fori_loop(0, nn, body, 0)
 
-    def put(g):
+    def put(g, par):
         outs[g] = []
+        n = len(GROUPS[g])
         for i, b in enumerate(GROUPS[g]):
             s = rel(b)
-            q = 4 * g + i
-            a = pltpu.make_async_copy(obuf.at[g % 2, pl.ds(i * CAP, CAP), :], os_ref.at[s], osem.at[q])
-            r = pltpu.make_async_remote_copy(obuf.at[g % 2, pl.ds((4 + i) * CAP, CAP), :], op_ref.at[s], pss.at[q],
-                                             prs.at[q], device_id=pos.target("P"), device_id_type=MESH)
+            a = pltpu.make_async_copy(obuf.at[par, pl.ds(i * CAP, CAP), :], os_ref.at[s], osem.at[s])
+            r = pltpu.make_async_remote_copy(obuf.at[par, pl.ds((n + i) * CAP, CAP), :], op_ref.at[s], pss.at[s],
+                                             prs.at[s], device_id=pos.target("P"), device_id_type=MESH)
             r.start()
             a.start()
             outs[g].append((a, r))
@@ -245,36 +250,26 @@
             a.wait()
             r.wait_send()
 
-    event(1)
+    half = (nf + 1) // 2
     lx.wait()
     lm.wait()
-    gather_rows(GROUPS[0])
-    up(0, True)
-    up(1, True)
-    event(2)
-    down(0, True)
-    put(0)
-    event(3)
-    gather_rows(GROUPS[1])
-    up(0, False)
-    up(1, False)
-    event(4)
-    down(1, False)
-    put(1)
-    gather_rows(GROUPS[2])
-    up(0, False)
-    event(5)
-    up(1, False)
-    put_done(0)
-    down(2, False)
-    put(2)
-    event(6)
-    gather_rows(GROUPS[3])
-    up(0, False)
-    up(1, False)
-    put_done(1)
-    down(3, False)
-    put(3)
+    for g, group in enumerate(GROUPS):
+        m = 2 * CAP * len(group)
+        before, early, late = WHEN[g].split("_")
+        for n in before:
+            event(int(n))
+        gather_rows(group)
+        up(m, 0, half, g == 0)
+        for n in early:
+            event(int(n))
+        up(m, half, nf, g == 0)
+        for n in late:
+            event(int(n))
+        if g >= 2:
+            put_done(g - 2)
+        down(m, g % 2, g == 0)
+        put(g, g % 2)
+    last = len(GROUPS)
     mo_ref[...] = mall[0]
     for n, make in enumerate(sends):
         def done(make=make):
@@ -284,25 +279,26 @@
             pl.when(pos.mid)(done)
         else:
             done()
-    put_done(2)
-    put_done(3)
-    for g in range(4):
+    put_done(last - 2)
+    put_done(last - 1)
+    for g in outs:
         for a, r in outs[g]:
             r.wait_recv()
 
 
-SLOTS = cut("dX3dX1dY2dY0cX0cX1cX2cX3cY0cY1cY2cY3az0az2az3bz0bz1", 3)
+SLOTS = cut("cX2cX0cY3cY1az0az2az3bz0bz1", 3)
+RAW = cut("dX3dX1dY2dY0cX3cX1cY2cY0", 3)
 HOPS = {"1": "bz1az0az0", "2": "az2bz1az3", "3": "az3bz0az2"}
 
 
 def combine_kernel(axes, os_ref, op_ref, m_ref, x_ref, v1_ref, v3_ref, v2_ref, y_ref,
-                   ov, sbuf, rbuf, w13, w2v, hs, sh, xv,
-                   osem, ssem, rsem, ws, w2s, ls):
+                   ov, sbuf, rbuf, raw, w13, w2v, hs, sh, xv,
+                   osem, ssem, rsem, us, ur, ws, w2s, ls):
     pos = Place(axes)
     t, hdim = x_ref.shape
     nf = v1_ref.shape[1] // 128
     nn = hdim // TN
-    order = [rel(b) for b in cut("D3D2D1D0X3Y3X2Y2X1Y1X0Y0C3C2C1C0", 2)]
+    order = [rel(b) for b in cut("D3D2X3Y3Y2X2D1X1D0C3C2Y1Y0X0C1C0", 2)]
 
     def o_copy(s, h):
         src = os_ref if h == 0 else op_ref
@@ -336,13 +332,44 @@
     barrier(pos)
     tri = strict_upper(t)
 
+    def spread(s, dev, rows):
+        a, _, _ = slots(m_ref[s], dev, tri)
+        b, _, _ = slots(m_ref[s], dev + 1 - 2 * pos.c, tri)
+        ab = jnp.concatenate([a, b], axis=0).T.astype(BF16)
+        return jnp.dot(ab, rows, preferred_element_type=F32)
+
+    loaded = set()
+
+    def load(s):
+        if s not in loaded:
+            o_copy(s, 0).wait()
+            o_copy(s, 1).wait()
+            loaded.add(s)
+
     def contrib(s):
-        o_copy(s, 0).wait()
-        o_copy(s, 1).wait()
-        a, _, _ = slots(m_ref[s], pos.me, tri)
-        b, _, _ = slots(m_ref[s], pos.mate, tri)
-        ab = jnp.concatenate([a, b], axis=0).T.astype(BF16)
-        return jnp.dot(ab, ov[s], preferred_element_type=F32)
+        load(s)
+        return spread(s, pos.me, ov[s])
+
+    uslot = {name: n for n, name in enumerate(RAW)}
+
+    def raw_copy(s, n, to):
+        return pltpu.make_async_remote_copy(ov.at[s], raw.at[n], us.at[n], ur.at[n],
+                                            device_id=pos.target(to), device_id_type=MESH)
+
+    rawsent = []
+
+    def pass_raw(b, to):
+        s = rel(b)
+        load(s)
+        n = uslot[("d" if b[0] == "D" else "c") + to + b[1]]
+        c = raw_copy(s, n, to)
+        c.start()
+        rawsent.append(c)
+
+    def got_raw(name, s):
+        n = uslot[name]
+        raw_copy(0, n, "X").wait_recv()
+        return spread(s, pos.chip[name[1]], raw[n])
 
     def copy(i, n, name):
         return pltpu.make_async_remote_copy(sbuf.at[i], rbuf.at[n], ssem.at[i], rsem.at[n],
@@ -362,15 +389,13 @@
         c.start()
         used.append(c)
 
-    for b, to in zip(cut("D3D2D1D0", 2), "XYXY"):
-        emit(contrib(rel(b)), "d" + to + b[1], to)
-
-    def column(k):
-        for to, other in (("X", "Y"), ("Y", "X")):
-            v = contrib(rel(to + k))
-            if "d" + other + k in slot:
-                v = v + got("d" + other + k)
-            emit(v, "c" + to + k, to)
+    def column(to, k):
+        s = rel(to + k)
+        other = "X" if to == "Y" else "Y"
+        emit(contrib(s) + got_raw("d" + other + k, s), "c" + to + k, to)
+
+    def part(name, s):
+        return got(name) if name in slot else got_raw(name, s)
 
     def share_up(lo, hi):
         def body(i, _):
@@ -389,34 +414,45 @@
             return 0
         lax.fori_loop(0, nn, body, 0)
 
-    zs = []
-
-    def along(k):
-        v = contrib(rel("C" + k)) + got("cX" + k) + got("cY" + k)
-        i = len(used) + len(zs)
+    zs = set()
+
+    def along(k, mid):
+        i = 3 + int(k)
+        load(rel("C" + k))
         mid_in, mid_to, end_to = cut(HOPS[k], 3)
-        link = "Z1" if mid_to[0] == "a" else "Z3"
-
-        @pl.when(pos.mid)
+
+        @pl.when(pos.mid if mid else jnp.logical_not(pos.mid))
         def _():
-            sbuf[i] = (v + got(mid_in)).astype(BF16)
-            copy(i, slot[mid_to], link).start()
-
-        @pl.when(jnp.logical_not(pos.mid))
-        def _():
+            s = rel("C" + k)
+            v = spread(s, pos.me, ov[s]) + part("cX" + k, s) + part("cY" + k, s)
+            if mid:
+                v = v + got(mid_in)
             sbuf[i] = v.astype(BF16)
-            copy(i, slot[end_to], "Z1").start()
-        zs.append(i)
-
-    for k in "3210":
-        column(k)
+            name = "Z3" if mid and mid_to[0] == "b" else "Z1"
+            copy(i, slot[mid_to if mid else end_to], name).start()
+        zs.add(i)
+
+    for b, to in zip(cut("D3D2X3", 2), "XYX"):
+        pass_raw(b, to)
+    column("Y", "3")
+    pass_raw("Y2", "Y")
+    column("X", "2")
+    for b, to in zip(cut("D1X1D0", 2), "XXY"):
+        pass_raw(b, to)
     lx.wait()
-    share_up(0, nf)
-    along("3")
+    share_up(0, nf // 2)
+    along("3", False)
+    share_up(nf // 2, nf)
+    along("2", False)
+    along("2", True)
+    column("Y", "1")
+    pass_raw("Y0", "Y")
+    column("X", "0")
     share_down()
-    along("2")
-    along("1")
-    v = sh[...] + contrib(rel("C0")) + got("cX0") + got("cY0") + got("az0")
+    along("3", True)
+    along("1", False)
+    along("1", True)
+    v = sh[...] + contrib(rel("C0")) + part("cX0", rel("C0")) + part("cY0", rel("C0")) + got("az0")
     sh[...] = v
 
     @pl.when(pos.mid)
@@ -426,7 +462,7 @@
     @pl.when(jnp.logical_not(pos.mid))
     def _():
         y_ref[...] = sh[...].astype(BF16)
-    for c in used:
+    for c in used + rawsent:
         c.wait_send()
     for i in zs:
         copy(i, 0, "X").wait_send()
@@ -449,7 +485,7 @@
         f = w1.shape[2]
         fs = ws1.shape[1]
         nch = mesh.size // 2
-        rows = 8 * CAP
+        rows = 2 * MOST * CAP
         pad = ((0, 8 - top), (0, 0))
         meta = jnp.concatenate([jnp.pad(ids.T.astype(F32), pad, constant_values=-1.0), jnp.pad(gates.T, pad)], axis=0)
         dma = pltpu.SemaphoreType.DMA
@@ -467,7 +503,7 @@
             scratch_shapes=[
                 pltpu.VMEM((2, nch, t, hdim), BF16),
                 pltpu.VMEM((2, nch, 16, t), F32),
-                pltpu.VMEM((2 * f // 128, hdim, 256), BF16),
+                pltpu.VMEM((f // 128, hdim, 512), BF16),
                 pltpu.VMEM((2 * hdim // TN, f, TN), BF16),
                 pltpu.VMEM((rows, hdim), BF16),
                 pltpu.VMEM((2, rows, f), BF16),
@@ -487,14 +523,15 @@
             out_specs=VM,
             scratch_shapes=[
                 pltpu.VMEM((nch, 2 * CAP, hdim), BF16),
-                pltpu.VMEM((15, t, hdim), BF16),
-                pltpu.VMEM((17, t, hdim), BF16),
+                pltpu.VMEM((7, t, hdim), BF16),
+                pltpu.VMEM((len(SLOTS), t, hdim), BF16),
+                pltpu.VMEM((len(RAW), 2 * CAP, hdim), BF16),
                 pltpu.VMEM((fs // 128, hdim, 256), BF16),
                 pltpu.VMEM((hdim // TN, fs, TN), BF16),
                 pltpu.VMEM((t, fs), BF16),
                 pltpu.VMEM((t, hdim), F32),
                 pltpu.VMEM((t, hdim), BF16),
-                dma((2, nch)), dma((15,)), dma((17,)),
+                dma((2, nch)), dma((7,)), dma((len(SLOTS),)), dma((len(RAW),)), dma((len(RAW),)),
                 dma((2, fs // 128)), dma((hdim // TN,)), dma((1,)),
             ],
             compiler_params=pltpu.CompilerParams(collective_id=1, has_side_effects=True, vmem_limit_bytes=VLIM),

time: 222 us -> 176 us (0.79)
  Pallas kernels: 218 us -> 172 us
    pallas_call x1, Pallas kernels: 98.7 us -> 68.8 us  [local(): pl.pallas_call(functools.partial(combine_kernel, axes), name='combine', o...]
    pallas_call x1, Pallas kernels: 119 us -> 103 us  [local(): pl.pallas_call(functools.partial(expert_kernel, axes), name='experts', ou...]
where the time goes in v2:
time: 176 us
  Pallas kernels  172 us (98%)
  other arithmetic  1.98 us (1%)
  local copies, waits for them, and re-layouts  1.88 us (1%)
    pallas_call x1, Pallas kernels, local(): pl.pallas_call(functools.partial(expert_kernel, axes), name='experts', ou...  103 us
    pallas_call x1, Pallas kernels, local(): pl.pallas_call(functools.partial(combine_kernel, axes), name='combine', o...  68.8 us

profile of v2, /device:TPU:0, one launch (start us, length us, event | category | flops | bytes accessed | tf_op | source)
XLA Modules:
  0.0 175.8 jit_solution(11902203506590373034)
XLA Ops:
  0.0 0.7 convert_bitcast_fusion
  0.7 1.3 select_maximum_fusion.m_ref
  2.0 103.1 %experts.1 = (bf16[16,48,2048]{2,1,0:T(8,128)(2,1)}, bf16[16,48,2048]{2,1,0:T(8,128)(2,1)}, f32[16,16,128]{2,1,0:T(8,128)}) custom-call(bf16[128,2048]{1,0:T(8,128)(2,1)} %x_ref.3, f32[16,128]{1,0:T(8,128)} %select_maximum_fusion.m_ref, bf16[2,2048,1408]{2,1,0:T(8,128)(2,1)} %w1_ref.1, bf16[2,2048,1408]{2,1,0:T(8,128)(2,1)} %w3_ref.1, ...), custom_call_target="tpu_custom_call" | custom-call | tf_op jit(solution)/shard_map/experts/pallas_call | solution.py:493
  105.1 68.8 %combine.1 = bf16[128,2048]{1,0:T(8,128)(2,1)} custom-call(bf16[16,48,2048]{2,1,0:T(8,128)(2,1)} %get-tuple-element.8.os_ref, bf16[16,48,2048]{2,1,0:T(8,128)(2,1)} %get-tuple-element.9.op_ref, f32[16,16,128]{2,1,0:T(8,128)} %get-tuple-element.10.m_ref, bf16[128,2048]{1,0:T(8,128)(2,1)} %x_ref.3, bf16[2048,2816]{1,0:T(8,128)(2,1)} %v1_ref.1, ...), custom_call_target="tpu_custom_call" | custom-call | tf_op jit(solution)/shard_map/combine/pallas_call | solution.py:518
  173.9 1.9 %copy.11 = bf16[128,2048]{1,0:T(8,128)(2,1)} copy(bf16[128,2048]{1,0:T(8,128)(2,1)} %combine.1) | data formatting | bytes 1048576

commit v3 on v2

--- a/solution.py
+++ b/solution.py
@@ -72,12 +72,9 @@
         pl.semaphore_wait(sem, 4)
 
 
-def slots(meta, dev, tri):
-    ids = meta[0:8, :]
-    gat = meta[8:16, :]
-    e0 = (2 * dev).astype(F32)
-    m0 = ids == e0
-    m1 = ids == e0 + 1.0
+def slots(ids, gat, dev, tri):
+    m0 = ids == 2 * dev
+    m1 = ids == 2 * dev + 1
     g0 = jnp.sum(jnp.where(m0, gat, 0.0), axis=0, keepdims=True)
     g1 = jnp.sum(jnp.where(m1, gat, 0.0), axis=0, keepdims=True)
     hit = jnp.sum(jnp.where(m0, 1.0, 0.0) + jnp.where(m1, 1.0, 0.0), axis=0, keepdims=True) > 0.5
@@ -94,8 +91,8 @@
     return jnp.where(a < b, 1.0, 0.0).astype(BF16)
 
 
-GROUPS = [cut(g, 2) for g in ("C0X0Y0C1", "X1Y1C2", "C3Y2D0", "X2D1X3Y3", "D2D3")]
-WHEN = ("1__2", "__3", "__4", "5__6", "__")
+GROUPS = [cut(g, 2) for g in ("C0", "X0Y0C1", "X1Y1C2", "C3Y2D0", "X2D1X3Y3", "D2D3")]
+WHEN = ("__1", "__2", "__3", "__4", "5__6", "__")
 EVENTS = {
     1: "C1XC1YC13C31Y0XY0PX0PC1P",
     2: "C2XC2YC21X1YX1PY1PC2P",
@@ -106,9 +103,9 @@
 }
 
 
-def expert_kernel(axes, x_ref, m_ref, w1_ref, w3_ref, w2_ref, os_ref, op_ref, mo_ref,
-                  xall, mall, w13, w2v, xg, hbuf, gbuf, obuf,
-                  xs, xr, ms, mr, ls, ws, w2s, osem, pss, prs):
+def expert_kernel(axes, x_ref, i_ref, m_ref, w1_ref, w3_ref, w2_ref, os_ref, op_ref, io_ref, mo_ref,
+                  xall, iall, mall, w13, w2v, xg, hbuf, gbuf, obuf,
+                  xs, xr, js, jr, ms, mr, ls, ws, w2s, osem, pss, prs):
     pos = Place(axes)
     t, hdim = x_ref.shape
     nf = w1_ref.shape[2] // 128
@@ -123,7 +120,7 @@
 
         def make():
             out = []
-            for ref, full, ss, rs in ((m_ref, mall, ms, mr), (x_ref, xall, xs, xr)):
+            for ref, full, ss, rs in ((i_ref, iall, js, jr), (m_ref, mall, ms, mr), (x_ref, xall, xs, xr)):
                 src = ref if own else full.at[0, rel(b)]
                 out.append(pltpu.make_async_remote_copy(src, full.at[dc, dst], ss.at[n], rs.at[dc, dst],
                                                         device_id=pos.target(name), device_id_type=MESH))
@@ -133,7 +130,7 @@
         sends.append(make)
 
     def arrived(b, dc):
-        for ref, full, ss, rs in ((m_ref, mall, ms, mr), (x_ref, xall, xs, xr)):
+        for ref, full, ss, rs in ((i_ref, iall, js, jr), (m_ref, mall, ms, mr), (x_ref, xall, xs, xr)):
             pltpu.make_async_remote_copy(ref, full.at[dc, rel(b)], ss.at[0], rs.at[dc, rel(b)],
                                          device_id=pos.target("X"), device_id_type=MESH).wait_recv()
 
@@ -149,8 +146,10 @@
     send("C0", "P", True)
     lx = pltpu.make_async_copy(x_ref, xall.at[0, 0], ls.at[0])
     lm = pltpu.make_async_copy(m_ref, mall.at[0, 0], ls.at[1])
+    li = pltpu.make_async_copy(i_ref, iall.at[0, 0], ls.at[2])
     lx.start()
     lm.start()
+    li.start()
 
     def w13_copy(i, half):
         e, j = i // nf, i % nf
@@ -200,7 +199,7 @@
             arrived(b, 1)
         for dc in range(2):
             for i, b in enumerate(group):
-                oh, g0, g1 = slots(mall[dc, rel(b)], pos.me, tri)
+                oh, g0, g1 = slots(iall[dc, rel(b)], mall[dc, rel(b)], pos.me, tri)
                 r0 = (dc * len(group) + i) * CAP
                 rows = slice(r0, r0 + CAP)
                 xg[rows, :] = jnp.dot(oh.astype(BF16), xall[dc, rel(b)], preferred_element_type=F32).astype(BF16)
@@ -253,6 +252,7 @@
     half = (nf + 1) // 2
     lx.wait()
     lm.wait()
+    li.wait()
     for g, group in enumerate(GROUPS):
         m = 2 * CAP * len(group)
         before, early, late = WHEN[g].split("_")
@@ -270,6 +270,7 @@
         down(m, g % 2, g == 0)
         put(g, g % 2)
     last = len(GROUPS)
+    io_ref[...] = iall[0]
     mo_ref[...] = mall[0]
     for n, make in enumerate(sends):
         def done(make=make):
@@ -291,7 +292,7 @@
 HOPS = {"1": "bz1az0az0", "2": "az2bz1az3", "3": "az3bz0az2"}
 
 
-def combine_kernel(axes, os_ref, op_ref, m_ref, x_ref, v1_ref, v3_ref, v2_ref, y_ref,
+def combine_kernel(axes, os_ref, op_ref, i_ref, m_ref, x_ref, v1_ref, v3_ref, v2_ref, y_ref,
                    ov, sbuf, rbuf, raw, w13, w2v, hs, sh, xv,
                    osem, ssem, rsem, us, ur, ws, w2s, ls):
     pos = Place(axes)
@@ -333,8 +334,8 @@
     tri = strict_upper(t)
 
     def spread(s, dev, rows):
-        a, _, _ = slots(m_ref[s], dev, tri)
-        b, _, _ = slots(m_ref[s], dev + 1 - 2 * pos.c, tri)
+        a, _, _ = slots(i_ref[s], m_ref[s], dev, tri)
+        b, _, _ = slots(i_ref[s], m_ref[s], dev + 1 - 2 * pos.c, tri)
         ab = jnp.concatenate([a, b], axis=0).T.astype(BF16)
         return jnp.dot(ab, rows, preferred_element_type=F32)
 
@@ -486,40 +487,40 @@
         fs = ws1.shape[1]
         nch = mesh.size // 2
         rows = 2 * MOST * CAP
-        pad = ((0, 8 - top), (0, 0))
-        meta = jnp.concatenate([jnp.pad(ids.T.astype(F32), pad, constant_values=-1.0), jnp.pad(gates.T, pad)], axis=0)
         dma = pltpu.SemaphoreType.DMA
         nsend = 40
-        o_same, o_mate, m_same = pl.pallas_call(
+        o_same, o_mate, i_same, m_same = pl.pallas_call(
             functools.partial(expert_kernel, axes),
             name="experts",
             out_shape=(
                 jax.ShapeDtypeStruct((nch, CAP, hdim), BF16),
                 jax.ShapeDtypeStruct((nch, CAP, hdim), BF16),
-                jax.ShapeDtypeStruct((nch, 16, t), F32),
+                jax.ShapeDtypeStruct((nch, top, t), jnp.int32),
+                jax.ShapeDtypeStruct((nch, top, t), F32),
             ),
-            in_specs=[ANY] * 5,
-            out_specs=(ANY, ANY, VM),
+            in_specs=[ANY] * 6,
+            out_specs=(ANY, ANY, VM, VM),
             scratch_shapes=[
                 pltpu.VMEM((2, nch, t, hdim), BF16),
-                pltpu.VMEM((2, nch, 16, t), F32),
+                pltpu.VMEM((2, nch, top, t), jnp.int32),
+                pltpu.VMEM((2, nch, top, t), F32),
                 pltpu.VMEM((f // 128, hdim, 512), BF16),
                 pltpu.VMEM((2 * hdim // TN, f, TN), BF16),
                 pltpu.VMEM((rows, hdim), BF16),
                 pltpu.VMEM((2, rows, f), BF16),
                 pltpu.VMEM((2, rows, 128), F32),
                 pltpu.VMEM((2, rows, hdim), BF16),
-                dma((nsend,)), dma((2, nch)), dma((nsend,)), dma((2, nch)),
-                dma((2,)), dma((2, 2 * f // 128)), dma((2 * hdim // TN,)),
+                dma((nsend,)), dma((2, nch)), dma((nsend,)), dma((2, nch)), dma((nsend,)), dma((2, nch)),
+                dma((3,)), dma((2, 2 * f // 128)), dma((2 * hdim // TN,)),
                 dma((nch,)), dma((nch,)), dma((nch,)),
             ],
             compiler_params=pltpu.CompilerParams(collective_id=0, has_side_effects=True, vmem_limit_bytes=VLIM),
-        )(x, meta, w1, w3, w2)
+        )(x, ids.T, gates.T, w1, w3, w2)
         y = pl.pallas_call(
             functools.partial(combine_kernel, axes),
             name="combine",
             out_shape=jax.ShapeDtypeStruct((t, hdim), BF16),
-            in_specs=[ANY, ANY, VM, ANY, ANY, ANY, ANY],
+            in_specs=[ANY, ANY, VM, VM, ANY, ANY, ANY, ANY],
             out_specs=VM,
             scratch_shapes=[
                 pltpu.VMEM((nch, 2 * CAP, hdim), BF16),
@@ -535,7 +536,7 @@
                 dma((2, fs // 128)), dma((hdim // TN,)), dma((1,)),
             ],
             compiler_params=pltpu.CompilerParams(collective_id=1, has_side_effects=True, vmem_limit_bytes=VLIM),
-        )(o_same, o_mate, m_same, x, ws1, ws3, ws2)
+        )(o_same, o_mate, i_same, m_same, x, ws1, ws3, ws2)
         return y
 
     return jax.shard_map(local, mesh=mesh, in_specs=(tok, tok, tok, wsp, wsp, wsp, rep, rep, rep), out_specs=tok, check_vma=False)

time: 176 us -> 172 us (0.977)
  Pallas kernels: 172 us -> 170 us
  other arithmetic: 1.98 us -> 0 us
where the time goes in v3:
time: 172 us
  Pallas kernels  170 us (99%)
  local copies, waits for them, and re-layouts  1.88 us (1%)
    pallas_call x1, Pallas kernels, local(): pl.pallas_call(functools.partial(expert_kernel, axes), name='experts', ou...  102 us
    pallas_call x1, Pallas kernels, local(): pl.pallas_call(functools.partial(combine_kernel, axes), name='combine', o...  68.1 us

profile of v3, /device:TPU:0, one launch (start us, length us, event | category | flops | bytes accessed | tf_op | source)
XLA Modules:
  0.0 171.9 jit_solution(3586331914118066907)
XLA Ops:
  0.0 101.9 %experts.1 = (bf16[16,48,2048]{2,1,0:T(8,128)(2,1)}, bf16[16,48,2048]{2,1,0:T(8,128)(2,1)}, s32[16,6,128]{2,1,0:T(8,128)}, f32[16,6,128]{2,1,0:T(8,128)}) custom-call(bf16[128,2048]{1,0:T(8,128)(2,1)} %x_ref.3, s32[6,128]{1,0:T(8,128)} %bitcast.2, f32[6,128]{1,0:T(8,128)} %bitcast.3, bf16[2,2048,1408]{2,1,0:T(8,128)(2,1)} %w1_ref.1, ...), custom_call_target="tpu_custom_call" | custom-call | tf_op jit(solution)/shard_map/experts/pallas_call | solution.py:492
  101.9 68.1 %combine.1 = bf16[128,2048]{1,0:T(8,128)(2,1)} custom-call(bf16[16,48,2048]{2,1,0:T(8,128)(2,1)} %get-tuple-element.9.os_ref, bf16[16,48,2048]{2,1,0:T(8,128)(2,1)} %get-tuple-element.10.op_ref, s32[16,6,128]{2,1,0:T(8,128)} %get-tuple-element.11.i_ref, f32[16,6,128]{2,1,0:T(8,128)} %get-tuple-element.12.m_ref, bf16[128,2048]{1,0:T(8,128)(2,1)} %x_ref.3, ...), custom_call_target="tpu_custom_call" | custom-call | tf_op jit(solution)/shard_map/combine/pallas_call | solution.py:519
  170.0 1.9 %copy.11 = bf16[128,2048]{1,0:T(8,128)(2,1)} copy(bf16[128,2048]{1,0:T(8,128)(2,1)} %combine.1) | data formatting | bytes 1048576
